TPU v7x, 128 devices: a whole 4x4x4 slice. The times are simulated.
128 devices in a mesh: rep: 8 (over y, x_hi), tp: 16 (over x_lo, z, core).
Axes of the slice: x: 4 (x_hi: 2, x_lo: 2; x = x_hi * 2 + x_lo), y: 4, z: 4, core: 2. Of those that a mesh axis runs over, the one named last changes fastest.
Arguments:
- hidden: bfloat16 [4096, 14336], P('rep'), may hold values from -6 to 6
- ln_gain: float32 [14336], replicated, may hold values from 0.1 to 1.9
- ln_shift: float32 [14336], replicated, may hold values from -3 to 3
- qkv_weight: bfloat16 [14336, 32, 384], P(('rep', 'tp')), may hold values from -0.046875 to 0.046875
- qkv_bias: float32 [32, 384], P('tp'), may hold values from -64 to 64
- out_weight: bfloat16 [14336, 32, 128], P('tp'), may hold values from -0.375 to 0.375
- out_bias: float32 [14336], P('tp'), may hold values from -3 to 3
- slope_index: int32 [32], P('tp'), may hold values from 0 to 111
Outputs:
- attended: bfloat16 [4096, 14336], P('rep', 'tp')
All inputs are finite; a program needn't handle non-finite values.
Results may differ from a plain program's by a relative error of at most 0.024.
The roundings to bfloat16 on the way count: a program that leaves them out, or rounds other values in their place, can miss the bound.
Values may be sent and summed in bfloat16 or wider, within the bound.
A program may use at most 192 MiB of HBM per device.

v0:
```python
import math
import jax
import jax.numpy as jnp
from jax import lax
from jax.sharding import PartitionSpec as P

N_SLOPES = 112
epsilon = 1e-05


def slope_values(slope_index):
    power = 1 << N_SLOPES.bit_length() - 1
    index_float = slope_index.astype(jnp.float32)
    leading = jnp.exp2(-8.0 * (index_float + 1.0) / power)
    between = jnp.exp2(-4.0 * (2.0 * (index_float - power) + 1.0) / power)
    return jnp.where(slope_index < power, leading, between)


def layer_norm(hidden, ln_gain, ln_shift):
    inputs_f32 = hidden.astype(jnp.float32)
    average = jnp.mean(inputs_f32, axis=-1, keepdims=True)
    centred = inputs_f32 - average
    variance = jnp.mean(centred * centred, axis=-1, keepdims=True)
    return (centred * lax.rsqrt(variance + epsilon) * ln_gain + ln_shift).astype(jnp.bfloat16)


def shards(hidden, ln_gain, ln_shift, qkv_weight, qkv_bias, out_weight, out_bias, slope_index):
    seq_rows = hidden.shape[0]
    heads_here = qkv_bias.shape[0]
    head_size = qkv_bias.shape[1] // 3
    flat_width = heads_here * 3 * head_size
    normed = layer_norm(hidden, ln_gain, ln_shift)
    regrouped = lax.all_to_all(qkv_weight, "tp", split_axis=1, concat_axis=0, tiled=True)
    weight_piece = lax.all_gather(regrouped, "rep", axis=0, tiled=True)
    flat_piece = weight_piece.reshape(weight_piece.shape[0], flat_width)
    projected = jnp.dot(normed, flat_piece, preferred_element_type=jnp.float32)
    qkv = (projected.reshape(seq_rows, heads_here, 3 * head_size) + qkv_bias).astype(jnp.bfloat16)
    query = qkv[:, :, :head_size]
    keys = qkv[:, :, head_size : 2 * head_size]
    values = qkv[:, :, 2 * head_size :]
    slopes = slope_values(slope_index)
    scores = jnp.einsum(
        "sha,tha->hst", query, keys, preferred_element_type=jnp.float32
    ) / math.sqrt(head_size)
    position = lax.iota(jnp.int32, seq_rows)
    distance = (position[:, None] - position[None, :]).astype(jnp.float32)
    scores = scores - slopes[:, None, None] * distance
    scores = jnp.where(distance >= 0.0, scores, -1e30)
    highest = jnp.max(scores, axis=-1, keepdims=True)
    powered = jnp.exp(scores - highest)
    attention = (powered / jnp.sum(powered, axis=-1, keepdims=True)).astype(jnp.bfloat16)
    context = jnp.einsum(
        "hst,tha->sha", attention, values, preferred_element_type=jnp.float32
    ).astype(jnp.bfloat16)
    context = context.reshape(seq_rows, heads_here * head_size)
    everything = lax.all_gather(context, "tp", axis=1, tiled=True)
    groups = lax.axis_size("tp")
    group_width = heads_here * head_size
    context_blocks = everything.reshape(seq_rows, groups, group_width)
    weight_blocks = out_weight.reshape(out_weight.shape[0], groups, group_width)
    partials = jnp.einsum(
        "sgk,dgk->gsd", context_blocks, weight_blocks, preferred_element_type=jnp.float32
    ).astype(jnp.bfloat16)
    partials = lax.optimization_barrier(partials)
    result = jnp.sum(partials.astype(jnp.float32), axis=0) + out_bias
    return result.astype(jnp.bfloat16)


def solution(mesh):
    return jax.shard_map(
        shards,
        mesh=mesh,
        in_specs=(
            P("rep", None),
            P(),
            P(),
            P(("rep", "tp"), None, None),
            P("tp", None),
            P("tp", None, None),
            P("tp"),
            P("tp"),
        ),
        out_specs=P("rep", "tp"),
        check_vma=False,
    )
```

profile of v0, /device:TPU:1, one launch (start us, length us, event | category | flops | bytes accessed | tf_op | source)
XLA Modules:
  0.0 399.7 jit_solution(10070072146498777757)
XLA Ops:
  6.5 0.0 all-gather.3.cloned.1.call-start
  6.5 2.8 copy.16
  9.3 41.7 %all_to_all.18 = bf16[112,32,384]{2,0,1:T(8,128)(2,1)S(1)} all-to-all(bf16[112,32,384]{2,0,1:T(8,128)(2,1)S(1)} %copy.16), channel_id=1, replica_groups=mesh['rep'=8,'tp'=16] {'tp'}, dimensions={1} | all-to-all | bytes 5505024 | tf_op jit(solution)/shard_map/all_to_all | solution.py:33
  51.0 1.8 copy.17
  52.8 0.0 copy-start.5
  52.8 0.0 all-gather.3.cloned.1.call-update
  52.9 0.0 all-gather.5.cloned.1.call-start
  52.9 0.2 broadcast_compare_fusion
  53.1 0.1 subtract_convert_fusion
  53.3 0.2 copy-done.5
  53.5 7.2 %convert_reduce_fusion = f32[512]{0:T(512)S(1)} fusion(bf16[512,14336]{1,0:T(8,128)(2,1)} %param.8), kind=kLoop, calls=%fused_computation.2 | loop fusion | flops 14679552 | bytes 14682112 | tf_op jit(solution)/shard_map/reduce_sum | solution.py:21
  60.7 11.6 %fusion.3 = f32[512]{0:T(512)S(1)} fusion(bf16[512,14336]{1,0:T(8,128)(2,1)} %param.8, f32[512]{0:T(512)S(1)} %broadcast_multiply_fusion), kind=kLoop, calls=%fused_computation.5 | loop fusion | flops 29359616 | bytes 14684160 | tf_op jit(solution)/shard_map/reduce_sum | solution.py:23
  72.3 0.0 copy-start.2
  72.3 0.0 copy-start.3
  72.3 0.0 copy-start.4
  72.3 208.5 %all-gather.3.cloned.1.call-done = bf16[14336,2,384]{2,0,1:T(8,128)(2,1)} async-done(((bf16[1792,2,384]{2,0,1:T(8,128)(2,1)}), bf16[14336,2,384]{2,0,1:T(8,128)(2,1)}) %all-gather.3.cloned.1.call-update) | async-done | bytes 22020112 | tf_op jit(solution)/shard_map/all_gather | solution.py:34
  280.8 26.1 %copy.18 = bf16[14336,2,384]{0,2,1:T(8,128)(2,1)} copy(bf16[14336,2,384]{2,0,1:T(8,128)(2,1)} %all-gather.3.cloned.1.call-done) | data formatting | bytes 44040192 | tf_op jit(solution)/shard_map/all_gather | solution.py:34
  306.9 0.0 copy-done.2
  306.9 0.0 copy-done.3
  306.9 0.0 copy-done.4
  306.9 17.8 %add_convert_fusion.1 = bf16[512,2,384]{2,0,1:T(8,128)(2,1)S(1)} fusion(bf16[14336,2,384]{0,2,1:T(8,128)(2,1)} %copy.18, bf16[512,14336]{1,0:T(8,128)(2,1)} %param.8, f32[14336]{0:T(1024)S(1)} %copy-done.2, f32[14336]{0:T(1024)S(1)} %copy-done.3, f32[512]{0:T(512)S(1)} %add_rsqrt_fusion, f32[512]{0:T(512)S(1)} %broadcast_multiply_fusion, ...), kind=kOutput, calls=%fused_computation.23 | convolution fusion | flops 11319115776 | bytes 37608448 | tf_op jit(solution)/shard_map/dot_general | solution.py:36
  324.7 0.0 copy-start
  324.7 0.9 copy-done
  325.6 0.6 subtract_select_fusion
  326.2 2.0 fusion.30
  328.2 2.3 convolution_convert_fusion.1
  330.5 0.0 all-gather.5.cloned.1.call-update
  330.6 11.5 %reshape.49 = bf16[896,16,256]{2,1,0:T(8,128)(2,1)} reshape(bf16[896,32,128]{2,1,0:T(8,128)(2,1)} %param.13) | data formatting | bytes 14680064 | tf_op jit(solution)/shard_map/reshape | solution.py:60
  342.0 25.0 %all-gather.5.cloned.1.call-done = bf16[512,4096]{0,1:T(8,128)(2,1)} async-done(((bf16[512,256]{0,1:T(8,128)(2,1)}), bf16[512,4096]{0,1:T(8,128)(2,1)}) %all-gather.5.cloned.1.call-update) | async-done | bytes 4194320 | tf_op jit(solution)/shard_map/all_gather | solution.py:56
  367.0 17.4 %convolution_convert_fusion = bf16[16,512,896]{2,1,0:T(8,128)(2,1)} fusion(bf16[512,16,256]{0,2,1:T(8,128)(2,1)} %bitcast.26, bf16[896,16,256]{2,1,0:T(8,128)(2,1)} %reshape.49), kind=kOutput, calls=%fused_computation.17 | convolution fusion | flops 3765436416 | bytes 26214400 | tf_op jit(solution)/shard_map/sgk,dgk->gsd/dot_general | solution.py:61
  384.4 0.0 copy-start.1
  384.4 7.4 %convert_reduce_fusion.1 = f32[512,896]{1,0:T(8,128)S(1)} fusion(bf16[16,512,896]{2,1,0:T(8,128)(2,1)} %convolution_convert_fusion), kind=kLoop, calls=%fused_computation.9 | loop fusion | flops 14221312 | bytes 16515072 | tf_op jit(solution)/shard_map/reduce_sum | solution.py:65
  391.8 0.0 copy-done.1
  391.8 1.0 add_convert_fusion
  (3 shorter events, 0.0 us)
Async XLA Ops:
  6.5 274.3 %all-gather.3.cloned.1.call-start = ((), (), s32[]{:S(2)}) async-start(), calls=%async_computation.1 | async-start | bytes 24772608 | tf_op jit(solution)/shard_map/all_gather | solution.py:34
  52.8 0.7 copy-start.5
  52.9 314.2 %all-gather.5.cloned.1.call-start = ((), (), s32[]{:S(2)}) async-start(), calls=%async_computation.2 | async-start | bytes 4456448 | tf_op jit(solution)/shard_map/all_gather | solution.py:56
  72.3 234.6 %copy-start.2 = (f32[14336]{0:T(1024)S(1)}, f32[14336]{0:T(1024)}, u32[]{:S(2)}) copy-start(f32[14336]{0:T(1024)} %param.10) | copy-start | bytes 172036
  72.3 234.6 %copy-start.3 = (f32[14336]{0:T(1024)S(1)}, f32[14336]{0:T(1024)}, u32[]{:S(2)}) copy-start(f32[14336]{0:T(1024)} %param.9) | copy-start | bytes 172036
  72.3 234.6 %copy-start.4 = (f32[2,384]{1,0:T(2,128)S(1)}, f32[2,384]{1,0:T(2,128)}, u32[]{:S(2)}) copy-start(f32[2,384]{1,0:T(2,128)} %param.12) | copy-start | bytes 9220
  324.7 0.9 copy-start
  384.4 7.4 %copy-start.1 = (f32[896]{0:T(1024)S(1)}, f32[896]{0:T(1024)}, u32[]{:S(2)}) copy-start(f32[896]{0:T(1024)} %param.14) | copy-start | bytes 10756
Sparse Core Ops, SparseCore 0:
  53.0 227.7 all-gather.2
  330.7 36.3 all-gather.4
where the time goes:
time: 401 us; the launch traced here: 400 us
  waiting for transfers between devices  233 us (58%)
  local copies, waits for them, and re-layouts  43.3 us (11%)
  blocking collectives  41.7 us (10%)
  matrix products  40.1 us (10%)
  other arithmetic  27.6 us (7%)
  between operations  13.5 us (3%)
    all_gather x1, waiting for transfers between devices, shards(): weight_piece = lax.all_gather(regrouped, 'rep', axis=0, tiled=True)  208 us
    all_to_all x1, blocking collectives, shards(): lax.all_to_all(qkv_weight, 'tp', split_axis=1, concat_axis=0, tiled=True)  41.7 us
    all_gather x1, local copies, waits for them, and re-layouts, shards(): weight_piece = lax.all_gather(regrouped, 'rep', axis=0, tiled=True)  26.1 us
    all_gather x1, waiting for transfers between devices, shards(): everything = lax.all_gather(context, 'tp', axis=1, tiled=True)  25 us
    dot_general x1, matrix products, shards(): projected = jnp.dot(normed, flat_piece, preferred_element_type=jnp.float32)  17.8 us
    dot_general x1, matrix products, shards(): jnp.einsum('sgk,dgk->gsd', context_blocks, weight_blocks, preferred_eleme...  17.4 us
    reduce_sum x1, other arithmetic, layer_norm(): variance = jnp.mean(centred * centred, axis=-1, keepdims=True)  11.6 us
    reshape x1, local copies, waits for them, and re-layouts, shards(): weight_blocks = out_weight.reshape(out_weight.shape[0], groups, group_width)  11.5 us
  transfers between devices with their start and end apart: 2, of which 2 were waited for; matrix products, arithmetic and copies ran while one was open for 8% of the time, Pallas kernels for 0%

commit v1 on v0

--- a/solution.py
+++ b/solution.py
@@ -53,7 +53,9 @@
         "hst,tha->sha", attention, values, preferred_element_type=jnp.float32
     ).astype(jnp.bfloat16)
     context = context.reshape(seq_rows, heads_here * head_size)
-    everything = lax.all_gather(context, "tp", axis=1, tiled=True)
+    everything = jnp.concatenate(
+        lax.all_to_all(jnp.stack([context] * lax.axis_size("tp")), "tp", 0, 0), axis=1
+    )
     groups = lax.axis_size("tp")
     group_width = heads_here * head_size
     context_blocks = everything.reshape(seq_rows, groups, group_width)

time: 401 us -> 433 us (1.080); the launches traced: 400 us -> 427 us
  waiting for transfers between devices: 233 us -> 253 us
  starting transfers between devices: 0.04 us -> 5.84 us
    all_to_all x0 -> x1, waiting for transfers between devices: none -> 44.7 us  [shards(): lax.all_to_all(jnp.stack([context] * lax.axis_size('tp')), 'tp', 0, 0)]
    all_gather x1 -> x0, waiting for transfers between devices: 25 us -> none  [shards(): everything = lax.all_gather(context, 'tp', axis=1, tiled=True)]
    all_to_all x0 -> x1, starting transfers between devices: none -> 5.84 us  [shards(): lax.all_to_all(jnp.stack([context] * lax.axis_size('tp')), 'tp', 0, 0)]
  transfers between devices with their start and end apart: 2 -> 2, of which waited for: 2 -> 2; matrix products, arithmetic and copies ran while one was open for 8% -> 7% of each run, Pallas kernels for 0% -> 0%
where the time goes in v1:
time: 433 us; the launch traced here: 427 us
  waiting for transfers between devices  253 us (58%)
  local copies, waits for them, and re-layouts  45.8 us (11%)
  blocking collectives  41.7 us (10%)
  matrix products  39.7 us (9%)
  other arithmetic  27.6 us (6%)
  between operations  13.5 us (3%)
  starting transfers between devices  5.84 us (1%)
    all_gather x1, waiting for transfers between devices, shards(): weight_piece = lax.all_gather(regrouped, 'rep', axis=0, tiled=True)  208 us
    all_to_all x1, waiting for transfers between devices, shards(): lax.all_to_all(jnp.stack([context] * lax.axis_size('tp')), 'tp', 0, 0)  44.7 us
    all_to_all x1, blocking collectives, shards(): lax.all_to_all(qkv_weight, 'tp', split_axis=1, concat_axis=0, tiled=True)  41.7 us
    all_gather x1, local copies, waits for them, and re-layouts, shards(): weight_piece = lax.all_gather(regrouped, 'rep', axis=0, tiled=True)  26.1 us
    dot_general x1, matrix products, shards(): projected = jnp.dot(normed, flat_piece, preferred_element_type=jnp.float32)  18 us
    dot_general x1, matrix products, shards(): jnp.einsum('sgk,dgk->gsd', context_blocks, weight_blocks, preferred_eleme...  17.5 us
    reduce_sum x1, other arithmetic, layer_norm(): variance = jnp.mean(centred * centred, axis=-1, keepdims=True)  11.6 us
    reshape x1, local copies, waits for them, and re-layouts, shards(): weight_blocks = out_weight.reshape(out_weight.shape[0], groups, group_width)  11.5 us
  transfers between devices with their start and end apart: 2, of which 2 were waited for; matrix products, arithmetic and copies ran while one was open for 7% of the time, Pallas kernels for 0%

profile of v1, /device:TPU:1, one launch (start us, length us, event | category | flops | bytes accessed | tf_op | source)
XLA Modules:
  0.0 427.4 jit_solution(4483350790455405103)
XLA Ops:
  6.5 0.0 all-gather.2.cloned.1.call-start
  6.5 2.8 copy.17
  9.3 41.7 %all_to_all.23 = bf16[112,32,384]{2,0,1:T(8,128)(2,1)S(1)} all-to-all(bf16[112,32,384]{2,0,1:T(8,128)(2,1)S(1)} %copy.17), channel_id=1, replica_groups=mesh['rep'=8,'tp'=16] {'tp'}, dimensions={1} | all-to-all | bytes 5505024 | tf_op jit(solution)/shard_map/all_to_all | solution.py:33
  51.0 1.8 copy.18
  52.8 0.0 copy-start.5
  52.8 0.0 all-gather.2.cloned.1.call-update
  52.9 0.2 broadcast_compare_fusion
  53.1 0.1 subtract_convert_fusion
  53.2 0.3 copy-done.5
  53.5 7.2 %convert_reduce_fusion = f32[512]{0:T(512)S(1)} fusion(bf16[512,14336]{1,0:T(8,128)(2,1)} %param.8), kind=kLoop, calls=%fused_computation.2 | loop fusion | flops 14679552 | bytes 14682112 | tf_op jit(solution)/shard_map/reduce_sum | solution.py:21
  60.7 11.6 %fusion.3 = f32[512]{0:T(512)S(1)} fusion(bf16[512,14336]{1,0:T(8,128)(2,1)} %param.8, f32[512]{0:T(512)S(1)} %broadcast_multiply_fusion), kind=kLoop, calls=%fused_computation.5 | loop fusion | flops 29359616 | bytes 14684160 | tf_op jit(solution)/shard_map/reduce_sum | solution.py:23
  72.3 0.0 copy-start.2
  72.3 0.0 copy-start.3
  72.3 0.0 copy-start.4
  72.3 208.5 %all-gather.2.cloned.1.call-done = bf16[14336,2,384]{2,0,1:T(8,128)(2,1)} async-done(((bf16[1792,2,384]{2,0,1:T(8,128)(2,1)}), bf16[14336,2,384]{2,0,1:T(8,128)(2,1)}) %all-gather.2.cloned.1.call-update) | async-done | bytes 22020112 | tf_op jit(solution)/shard_map/all_gather | solution.py:34
  280.8 26.1 %copy.19 = bf16[14336,2,384]{0,2,1:T(8,128)(2,1)} copy(bf16[14336,2,384]{2,0,1:T(8,128)(2,1)} %all-gather.2.cloned.1.call-done) | data formatting | bytes 44040192 | tf_op jit(solution)/shard_map/all_gather | solution.py:34
  306.9 0.0 copy-done.2
  306.9 0.0 copy-done.3
  306.9 0.0 copy-done.4
  306.9 18.0 %add_convert_fusion.1 = bf16[512,2,384]{2,0,1:T(8,128)(2,1)S(1)} fusion(bf16[14336,2,384]{0,2,1:T(8,128)(2,1)} %copy.19, bf16[512,14336]{1,0:T(8,128)(2,1)} %param.8, f32[14336]{0:T(1024)S(1)} %copy-done.2, f32[14336]{0:T(1024)S(1)} %copy-done.3, f32[512]{0:T(512)S(1)} %add_rsqrt_fusion, f32[512]{0:T(512)S(1)} %broadcast_multiply_fusion, ...), kind=kOutput, calls=%fused_computation.24 | convolution fusion | flops 11319115776 | bytes 37608448 | tf_op jit(solution)/shard_map/dot_general | solution.py:36
  324.9 0.0 copy-start
  324.9 0.9 copy-done
  325.8 0.6 subtract_select_fusion
  326.4 2.1 fusion.31
  328.4 1.6 convolution_convert_fusion.1
  330.0 0.1 copy.22
  330.2 2.3 stack.3
  332.5 5.8 %all-to-all-start.1 = ((bf16[16,512,256]{2,1,0:T(8,128)(2,1)}), bf16[16,512,256]{2,1,0:T(8,128)(2,1)}, u32[]{:S(2)}, u32[]{:S(2)}) async-start(bf16[16,512,256]{2,1,0:T(8,128)(2,1)} %stack.3), calls=%async_computation.1 | async-start | bytes 8388608 | tf_op jit(solution)/shard_map/all_to_all | solution.py:57
  338.3 11.5 %reshape.47 = bf16[896,16,256]{2,1,0:T(8,128)(2,1)} reshape(bf16[896,32,128]{2,1,0:T(8,128)(2,1)} %param.13) | data formatting | bytes 14680064 | tf_op jit(solution)/shard_map/reshape | solution.py:62
  349.8 44.7 %all-to-all-done.1 = bf16[16,512,256]{2,1,0:T(8,128)(2,1)} async-done(((bf16[16,512,256]{2,1,0:T(8,128)(2,1)}), bf16[16,512,256]{2,1,0:T(8,128)(2,1)}, u32[]{:S(2)}, u32[]{:S(2)}) %all-to-all-start.1) | async-done | bytes 4194336 | tf_op jit(solution)/shard_map/all_to_all | solution.py:57
  394.6 17.5 %convolution_convert_fusion = bf16[16,512,896]{2,1,0:T(8,128)(2,1)} fusion(bf16[896,16,256]{2,1,0:T(8,128)(2,1)} %reshape.47, bf16[16,512,256]{2,1,0:T(8,128)(2,1)} %all-to-all-done.1), kind=kOutput, calls=%fused_computation.17 | convolution fusion | flops 3765436416 | bytes 26214400 | tf_op jit(solution)/shard_map/sgk,dgk->gsd/dot_general | solution.py:63
  412.1 0.0 copy-start.1
  412.1 7.4 %convert_reduce_fusion.1 = f32[512,896]{1,0:T(8,128)S(1)} fusion(bf16[16,512,896]{2,1,0:T(8,128)(2,1)} %convolution_convert_fusion), kind=kLoop, calls=%fused_computation.9 | loop fusion | flops 14221312 | bytes 16515072 | tf_op jit(solution)/shard_map/reduce_sum | solution.py:67
  419.5 0.0 copy-done.1
  419.5 1.0 add_convert_fusion
  (3 shorter events, 0.0 us)
Async XLA Ops:
  6.5 274.3 %all-gather.2.cloned.1.call-start = ((), (), s32[]{:S(2)}) async-start(), calls=%async_computation.2 | async-start | bytes 24772608 | tf_op jit(solution)/shard_map/all_gather | solution.py:34
  52.8 0.7 copy-start.5
  72.3 234.6 %copy-start.2 = (f32[14336]{0:T(1024)S(1)}, f32[14336]{0:T(1024)}, u32[]{:S(2)}) copy-start(f32[14336]{0:T(1024)} %param.10) | copy-start | bytes 172036
  72.3 234.6 %copy-start.3 = (f32[14336]{0:T(1024)S(1)}, f32[14336]{0:T(1024)}, u32[]{:S(2)}) copy-start(f32[14336]{0:T(1024)} %param.9) | copy-start | bytes 172036
  72.3 234.6 %copy-start.4 = (f32[2,384]{1,0:T(2,128)S(1)}, f32[2,384]{1,0:T(2,128)}, u32[]{:S(2)}) copy-start(f32[2,384]{1,0:T(2,128)} %param.12) | copy-start | bytes 9220
  324.9 0.9 copy-start
  332.5 62.0 %all-to-all-start.1 = ((bf16[16,512,256]{2,1,0:T(8,128)(2,1)}), bf16[16,512,256]{2,1,0:T(8,128)(2,1)}, u32[]{:S(2)}, u32[]{:S(2)}) async-start(bf16[16,512,256]{2,1,0:T(8,128)(2,1)} %stack.3), calls=%async_computation.1 | async-start | bytes 8388608 | tf_op jit(solution)/shard_map/all_to_all | solution.py:57
  412.1 7.4 %copy-start.1 = (f32[896]{0:T(1024)S(1)}, f32[896]{0:T(1024)}, u32[]{:S(2)}) copy-start(f32[896]{0:T(1024)} %param.14) | copy-start | bytes 10756
Sparse Core Ops, SparseCore 0:
  53.0 227.7 all-gather.1
